TPU v7x, 32 devices: a whole 2x2x4 slice. The times are simulated.
32 devices in a mesh: seq: 8 (over z, core), batch: 4 (over y, x).
Axes of the slice: x: 2, y: 2, z: 4, core: 2. Of those that a mesh axis runs over, the one named last changes fastest.
Arguments:
- tokens: bfloat16 [4, 2048, 1152], P('batch', 'seq'), may hold values from -6 to 6
- long_skip: bfloat16 [4, 2048, 1152], P('batch', 'seq'), may hold values from -6 to 6
- lengths: int32 [4, 4], P('batch'), may hold values from 0 to 1026, as said below
- skip_weight: bfloat16 [2304, 1152], replicated, may hold values from -0.125 to 0.125
- skip_bias: bfloat16 [1152], replicated, may hold values from -3 to 3
- attention_gain: bfloat16 [1152], replicated, may hold values from 0.099609375 to 1.8984375
- attention_shift: bfloat16 [1152], replicated, may hold values from -3 to 3
- qkv_weight: bfloat16 [1152, 3456], replicated, may hold values from -0.1875 to 0.1875
- out_weight: bfloat16 [1152, 1152], replicated, may hold values from -2 to 2
- out_bias: bfloat16 [1152], replicated, may hold values from -3 to 3
- mlp_gain: bfloat16 [1152], replicated, may hold values from 0.099609375 to 1.8984375
- mlp_shift: bfloat16 [1152], replicated, may hold values from -3 to 3
- hidden_weight: bfloat16 [1152, 4608], replicated, may hold values from -0.1875 to 0.1875
- hidden_bias: bfloat16 [4608], replicated, may hold values from -3 to 3
- down_weight: bfloat16 [4608, 1152], replicated, may hold values from -0.09375 to 0.09375
- down_bias: bfloat16 [1152], replicated, may hold values from -3 to 3
- cotangent: bfloat16 [4, 2048, 1152], P('batch', 'seq'), may hold values from -6 to 6
Outputs:
- output: bfloat16 [4, 2048, 1152], P('batch', 'seq')
- grad_tokens: float32 [4, 2048, 1152], P('batch', 'seq')
- grad_long_skip: float32 [4, 2048, 1152], P('batch', 'seq')
- grad_skip_weight: float32 [2304, 1152], P('batch', 'seq')
- grad_skip_bias: float32 [1152], replicated
- grad_attention_gain: float32 [1152], replicated
- grad_attention_shift: float32 [1152], replicated
- grad_qkv_weight: float32 [1152, 3456], P('batch', 'seq')
- grad_out_weight: float32 [1152, 1152], P('batch', 'seq')
- grad_out_bias: float32 [1152], replicated
- grad_mlp_gain: float32 [1152], replicated
- grad_mlp_shift: float32 [1152], replicated
- grad_hidden_weight: float32 [1152, 4608], P('batch', 'seq')
- grad_hidden_bias: float32 [4608], replicated
- grad_down_weight: float32 [4608, 1152], P('batch', 'seq')
- grad_down_bias: float32 [1152], replicated
Inputs may be any that keep to these rules, and one draw needn't show every extreme that they name: Row g lists the lengths of group g's items in the order in which they lie along the group's 2048 positions. Each entry is 258, 1026 or 0, every row has one or more entries 1026, zeros stand only after the last nonzero entry, and the row's total leaves fewer than 258 positions of padding at the end.
All inputs are finite; a program needn't handle non-finite values.
Results may differ from a plain program's by a relative error of at most 0.013.
Values may be sent and summed in bfloat16 or wider, within the bound.
A program may use at most 256 MiB of HBM per device.

v0:
```python
import math
import jax
import jax.numpy as jnp
from jax import lax
from jax.sharding import PartitionSpec as P

HD = 72
norm_eps = 1e-05


def product(left, right):
    return jnp.dot(left, right, preferred_element_type=jnp.float32)


def contract_rows(left, right):
    return lax.dot_general(
        left, right, (((0,), (0,)), ((), ())), preferred_element_type=jnp.float32
    )


def times_transposed(left, right):
    return lax.dot_general(
        left, right, (((1,), (1,)), ((), ())), preferred_element_type=jnp.float32
    )


def column_sums(values):
    return jnp.sum(values.astype(jnp.float32), axis=0)


def layer_norm(inputs, gain, shift):
    mean_row = jnp.mean(inputs, axis=-1, keepdims=True)
    centred = inputs - mean_row
    spread = jnp.mean(centred * centred, axis=-1, keepdims=True)
    return centred * lax.rsqrt(spread + norm_eps) * gain + shift


def exact_gelu(inputs):
    return jax.nn.gelu(inputs, approximate=False)


def segments(row_lengths, group_len):
    ends = jnp.cumsum(row_lengths)
    places = jnp.arange(group_len, dtype=jnp.int32)
    return jnp.sum((places[:, None] >= ends[None, :]).astype(jnp.int32), axis=1)


def score_block(query_block, key_heads, seg_block, segment):
    raw = jnp.einsum("bhd,khd->hbk", query_block, key_heads, preferred_element_type=jnp.float32)
    scores = raw * (1.0 / math.sqrt(HD))
    allowed = (seg_block[:, None] == segment[None, :])[None]
    return jnp.where(allowed, scores, -jnp.inf)


def attend_forward(query_heads, key_flat, value_flat, segment):
    length, head_cols = query_heads.shape
    head_count = head_cols // HD
    block_rows = min(512, length)
    block_count = length // block_rows
    key_heads = key_flat.reshape(length, head_count, HD)
    value_heads = value_flat.reshape(length, head_count, HD)

    def one_block(pieces):
        query_block, seg_block = pieces
        scores = score_block(query_block, key_heads, seg_block, segment)
        row_max = jnp.max(scores, axis=2, keepdims=True)
        log_total = row_max + jnp.log(jnp.sum(jnp.exp(scores - row_max), axis=2, keepdims=True))
        probs_low = jnp.exp(scores - log_total).astype(jnp.bfloat16)
        context = jnp.einsum(
            "hbk,khd->bhd", probs_low, value_heads, preferred_element_type=jnp.float32
        )
        return (context.astype(jnp.bfloat16).reshape(block_rows, head_cols), log_total)

    context, log_total = lax.map(
        one_block,
        (
            query_heads.reshape(block_count, block_rows, head_count, HD),
            segment.reshape(block_count, block_rows),
        ),
    )
    return (context.reshape(length, head_cols), log_total)


def attend_backward(query_heads, key_flat, value_flat, segment, grad_context, log_total):
    length, head_cols = query_heads.shape
    head_count = head_cols // HD
    block_rows = min(512, length)
    block_count = length // block_rows
    score_scale = 1.0 / math.sqrt(HD)
    key_heads = key_flat.reshape(length, head_count, HD)
    value_heads = value_flat.reshape(length, head_count, HD)

    def one_block(totals, pieces):
        grad_keys, grad_values = totals
        query_block, seg_block, grad_block, total_block = pieces
        scores = score_block(query_block, key_heads, seg_block, segment)
        prob_full = jnp.exp(scores - total_block)
        probs_low = prob_full.astype(jnp.bfloat16)
        grad_values = grad_values + jnp.einsum(
            "hbk,bhd->khd", probs_low, grad_block, preferred_element_type=jnp.float32
        )
        grad_probs = jnp.einsum(
            "bhd,khd->hbk", grad_block, value_heads, preferred_element_type=jnp.float32
        )
        row_delta = jnp.sum(prob_full * grad_probs, axis=2, keepdims=True)
        grad_scores = (prob_full * (grad_probs - row_delta)).astype(jnp.bfloat16)
        grad_query = (
            jnp.einsum("hbk,khd->bhd", grad_scores, key_heads, preferred_element_type=jnp.float32)
            * score_scale
        )
        grad_keys = grad_keys + jnp.einsum(
            "hbk,bhd->khd", grad_scores, query_block, preferred_element_type=jnp.float32
        )
        return (
            (grad_keys, grad_values),
            grad_query.astype(jnp.bfloat16).reshape(block_rows, head_cols),
        )

    empty_sum = jnp.zeros((length, head_count, HD), jnp.float32)
    (grad_keys, grad_values), grad_query = lax.scan(
        one_block,
        (empty_sum, empty_sum),
        (
            query_heads.reshape(block_count, block_rows, head_count, HD),
            segment.reshape(block_count, block_rows),
            grad_context.reshape(block_count, block_rows, head_count, HD),
            log_total,
        ),
    )
    grad_keys = (grad_keys * score_scale).astype(jnp.bfloat16).reshape(length, head_cols)
    grad_values = grad_values.astype(jnp.bfloat16).reshape(length, head_cols)
    return (grad_query.reshape(length, head_cols), grad_keys, grad_values)


def exchange(blocks, axis):
    count = blocks.shape[0]
    me = lax.axis_index(axis)
    got = [lax.dynamic_index_in_dim(blocks, me, axis=0, keepdims=False)]
    for step in range(1, count):
        piece = lax.dynamic_index_in_dim(blocks, (me + step) % count, axis=0, keepdims=False)
        pairs = [(source, (source + step) % count) for source in range(count)]
        got.append(lax.ppermute(piece, axis, pairs))
    order = (me - jnp.arange(count)) % count
    return jnp.take(jnp.stack(got), order, axis=0)


def split_columns(values, axis):
    count = lax.axis_size(axis)
    rows, cols = values.shape
    blocks = values.reshape(rows, count, cols // count).transpose(1, 0, 2)
    return exchange(blocks, axis).reshape(count * rows, cols // count)


def seq_gathered_grad(left, right):
    left_all = lax.all_gather(left, "seq", axis=0, tiled=True)
    right_cols = split_columns(right, "seq")
    partial = contract_rows(left_all, right_cols)
    return lax.psum_scatter(partial, "batch", scatter_dimension=0, tiled=True)


def batch_gathered_grad(left, right):
    left_rows = split_columns(left, "batch")
    right_all = lax.all_gather(right, "batch", axis=0, tiled=True)
    partial = contract_rows(left_rows, right_all)
    return lax.psum_scatter(partial, "seq", scatter_dimension=1, tiled=True)


GRAD_PLAN = {"skip": "batch", "qkv": "seq", "out": "batch", "hidden": "seq", "down": "batch"}


def weight_grad(name, left, right):
    if GRAD_PLAN[name] == "seq":
        return seq_gathered_grad(left, right)
    return batch_gathered_grad(left, right)


def on_device(
    tokens,
    long_skip,
    lengths,
    skip_weight,
    skip_bias,
    attention_gain,
    attention_shift,
    qkv_weight,
    out_weight,
    out_bias,
    mlp_gain,
    mlp_shift,
    hidden_weight,
    hidden_bias,
    down_weight,
    down_bias,
    cotangent,
):
    local_rows = tokens.shape[1]
    feature_count = tokens.shape[2]
    group_len = local_rows * lax.axis_size("seq")
    joined = jnp.concatenate([tokens[0], long_skip[0]], axis=1)
    mixed = product(joined, skip_weight) + skip_bias.astype(jnp.float32)
    normed_full, first_pull = jax.vjp(
        layer_norm, mixed, attention_gain.astype(jnp.float32), attention_shift.astype(jnp.float32)
    )
    normed_one = normed_full.astype(jnp.bfloat16)
    packed = product(normed_one, qkv_weight).astype(jnp.bfloat16)
    seq_count = lax.axis_size("seq")
    packed_heads = lax.all_to_all(
        packed.reshape(local_rows, 3, seq_count, feature_count // seq_count),
        "seq",
        split_axis=2,
        concat_axis=0,
        tiled=True,
    ).reshape(group_len, 3, feature_count // seq_count)
    query_heads = packed_heads[:, 0]
    key_heads = packed_heads[:, 1]
    value_heads = packed_heads[:, 2]
    segment = segments(lengths[0], group_len)
    context_heads, log_total = attend_forward(query_heads, key_heads, value_heads, segment)
    context_tok = lax.all_to_all(context_heads, "seq", split_axis=0, concat_axis=1, tiled=True)
    middle = mixed + product(context_tok, out_weight) + out_bias.astype(jnp.float32)
    second_full, second_pull = jax.vjp(
        layer_norm, middle, mlp_gain.astype(jnp.float32), mlp_shift.astype(jnp.float32)
    )
    normed_two = second_full.astype(jnp.bfloat16)
    hidden_pre = product(normed_two, hidden_weight) + hidden_bias.astype(jnp.float32)
    act_full, gelu_pull = jax.vjp(exact_gelu, hidden_pre)
    hidden_act = act_full.astype(jnp.bfloat16)
    output = (middle + product(hidden_act, down_weight) + down_bias.astype(jnp.float32)).astype(
        jnp.bfloat16
    )
    grad_out_rows = cotangent[0]
    grad_down_weight = weight_grad("down", hidden_act, grad_out_rows)
    grad_down_bias = column_sums(grad_out_rows)
    grad_act = times_transposed(grad_out_rows, down_weight)
    grad_pre = gelu_pull(grad_act)[0].astype(jnp.bfloat16)
    grad_hidden_weight = weight_grad("hidden", normed_two, grad_pre)
    grad_hidden_bias = column_sums(grad_pre)
    grad_normed_two = times_transposed(grad_pre, hidden_weight)
    grad_middle_norm, grad_mlp_gain, grad_mlp_shift = second_pull(grad_normed_two)
    grad_middle = grad_out_rows.astype(jnp.float32) + grad_middle_norm
    grad_attended = grad_middle.astype(jnp.bfloat16)
    grad_out_bias = column_sums(grad_attended)
    grad_out_weight = weight_grad("out", context_tok, grad_attended)
    grad_context = times_transposed(grad_attended, out_weight).astype(jnp.bfloat16)
    grad_context_heads = lax.all_to_all(
        grad_context, "seq", split_axis=1, concat_axis=0, tiled=True
    )
    grad_query, grad_key, grad_value = attend_backward(
        query_heads, key_heads, value_heads, segment, grad_context_heads, log_total
    )
    grad_packed = lax.all_to_all(
        jnp.stack([grad_query, grad_key, grad_value], axis=1)[:, :, None],
        "seq",
        split_axis=0,
        concat_axis=2,
        tiled=True,
    ).reshape(local_rows, 3 * feature_count)
    grad_qkv_weight = weight_grad("qkv", normed_one, grad_packed)
    grad_normed_one = times_transposed(grad_packed, qkv_weight)
    grad_mixed_norm, grad_attention_gain, grad_attention_shift = first_pull(grad_normed_one)
    grad_mixed = (grad_middle + grad_mixed_norm).astype(jnp.bfloat16)
    grad_skip_bias = column_sums(grad_mixed)
    grad_skip_weight = weight_grad("skip", joined, grad_mixed)
    grad_joined = times_transposed(grad_mixed, skip_weight)
    grad_tokens = grad_joined[:, :feature_count][None]
    grad_long_skip = grad_joined[:, feature_count:][None]
    summed_weights = (
        grad_skip_weight,
        grad_qkv_weight,
        grad_out_weight,
        grad_hidden_weight,
        grad_down_weight,
    )
    small_grads = (
        grad_skip_bias,
        grad_attention_gain,
        grad_attention_shift,
        grad_out_bias,
        grad_mlp_gain,
        grad_mlp_shift,
        grad_hidden_bias,
        grad_down_bias,
    )
    small_sizes = [piece.shape[0] for piece in small_grads]
    small_total = lax.psum(jnp.concatenate(small_grads), ("seq", "batch"))
    summed_small = []
    offset = 0
    for size in small_sizes:
        summed_small.append(small_total[offset : offset + size])
        offset += size
    return (
        output[None],
        grad_tokens,
        grad_long_skip,
        summed_weights[0],
        summed_small[0],
        summed_small[1],
        summed_small[2],
        summed_weights[1],
        summed_weights[2],
        summed_small[3],
        summed_small[4],
        summed_small[5],
        summed_weights[3],
        summed_small[6],
        summed_weights[4],
        summed_small[7],
    )


def solution(mesh):
    in_specs = (
        P("batch", "seq", None),
        P("batch", "seq", None),
        P("batch", None),
        P(),
        P(),
        P(),
        P(),
        P(),
        P(),
        P(),
        P(),
        P(),
        P(),
        P(),
        P(),
        P(),
        P("batch", "seq", None),
    )
    out_specs = (
        P("batch", "seq", None),
        P("batch", "seq", None),
        P("batch", "seq", None),
        P("batch", "seq"),
        P(),
        P(),
        P(),
        P("batch", "seq"),
        P("batch", "seq"),
        P(),
        P(),
        P(),
        P("batch", "seq"),
        P(),
        P("batch", "seq"),
        P(),
    )
    return jax.shard_map(
        on_device, mesh=mesh, in_specs=in_specs, out_specs=out_specs, check_vma=False
    )
```

profile of v0, /device:TPU:0, one launch (start us, length us, event | category | flops | bytes accessed | tf_op | source)
XLA Modules:
  0.0 813.6 jit_solution(7529825776939285861)
XLA Ops:
  14.6 7.2 convolution_convert_fusion
  28.5 6.8 all-to-all-start
  35.6 41.7 %all-to-all-done = bf16[256,3,8,144]{0,3,1,2:T(8,128)(2,1)} async-done(((bf16[256,3,8,144]{0,3,1,2:T(8,128)(2,1)}), bf16[256,3,8,144]{0,3,1,2:T(8,128)(2,1)}, u32[]{:S(2)}, u32[]{:S(2)}) %all-to-all-start) | async-done | bytes 1769504 | tf_op jit(solution)/shard_map/all_to_all | solution.py:207
  92.6 36.5 %while.27 = (s32[]{:T(128)}, bf16[4,512,144]{1,2,0:T(8,128)(2,1)}, f32[4,2,512,1]{2,1,3,0:T(2,128)S(1)}, s32[4,512]{1,0:T(4,128)S(1)}, s32[2048]{0:T(1024)S(1)},...) while((s32[]{:T(128)}, bf16[4,512,144]{1,2,0:T(8,128)(2,1)}, ...), condition=%wide.region_7.8_spmd, body=%wide.region_4.7_spmd.sunk | while | flops 628169728 | bytes 33537152 | solution.py:74
  140.6 16.1 %all-to-all-done.1 = bf16[8,256,144]{1,2,0:T(8,128)(2,1)} async-done(((bf16[8,256,144]{1,2,0:T(8,128)(2,1)}), bf16[8,256,144]{1,2,0:T(8,128)(2,1)}, u32[]{:S(2)}, u32[]{:S(2)}) %all-to-all-start.1) | async-done | bytes 589856 | tf_op jit(solution)/shard_map/all_to_all | solution.py:219
  161.4 17.1 %multiply_convert_fusion.1 = (bf16[256,4608]{1,0:T(8,128)(2,1)}, f32[256,4608]{1,0:T(8,128)}, f32[256,4608]{1,0:T(8,128)}) fusion(f32[4608]{0:T(1024)S(1)} %convert_element_type.104, bf16[256,1152]{1,0:T(8,128)(2,1)} %add_convert_fusion.2, bf16[1152,4608]{1,0:T(8,128)(2,1)} %param.33), kind=kOutput, calls=%fused_computation.61 | convolution fusion | flops 2795765760 | bytes 23021568 | tf_op jit(solution)/shard_map/dot_general | solution.py:12
  178.5 14.6 %convert_reduce_fusion = (f32[4608]{0:T(1024)}, bf16[256,4608]{1,0:T(8,128)(2,1)}) fusion(f32[256,4608]{1,0:T(8,128)} %get-tuple-element.309, f32[256,4608]{1,0:T(8,128)} %get-tuple-element.357, bf16[4608,1152]{1,0:T(8,128)(2,1)} %param.35, bf16[1,256,1152]{2,1,0:T(8,128)(2,1)S(1)} %copy-done.13), kind=kOutput, calls=%fused_computation.59 | convolution fusion | flops 2736778752 | bytes 23021568 | tf_op jit(solution)/shard_map/dot_general | solution.py:22
  193.2 8.7 %multiply_reduce_fusion.1 = (f32[1152]{0:T(1024)}, f32[256]{0:T(256)S(1)}, f32[1152]{0:T(1024)}, f32[256,1152]{1,0:T(8,128)S(1)}) fusion(f32[256,1152]{1,0:T(8,128)S(1)} %copy-done.7, f32[256]{0:T(256)S(1)} %fusion.83, f32[256]{0:T(256)S(1)} %broadcast_multiply_fusion, f32[1152]{0:T(1024)S(1)} %convert_element_type.101, ...), kind=kOutput, calls=%fused_computation.113 | convolution fusion | flops 2720265728 | bytes 15352320 | tf_op jit(solution)/shard_map/dot_general | solution.py:22
  214.5 15.9 %all-to-all-done.2 = bf16[256,8,144]{0,2,1:T(8,128)(2,1)S(1)} async-done(((bf16[256,8,144]{0,2,1:T(8,128)(2,1)}), bf16[256,8,144]{0,2,1:T(8,128)(2,1)S(1)}, u32[]{:S(2)}, u32[]{:S(2)}) %all-to-all-start.2) | async-done | bytes 589856 | tf_op jit(solution)/shard_map/all_to_all | solution.py:245
  232.7 96.8 %while.28 = (s32[]{:T(128)}, f32[2048,2,72]{0,2,1:T(8,128)S(1)}, f32[2048,2,72]{0,2,1:T(8,128)}, bf16[4,512,144]{1,2,0:T(8,128)(2,1)}, bf16[4,512,2,72]{1,3,2,0:...) while((s32[]{:T(128)}, f32[2048,2,72]{0,2,1:T(8,128)S(1)}, ...), condition=%wide.region_14.15_spmd.clone, body=%wide.region_12.14_spmd.clone.sunk | while | flops 1543781376 | bytes 144143088 | solution.py:120
  337.9 8.6 %reshape.483 = bf16[8,2,55296]{2,1,0:T(2,128)(2,1)} reshape(bf16[2048,1,3,144]{3,2,1,0:T(4,128)(2,1)} %bitcast.291) | data formatting | bytes 3538944
  351.0 41.1 %all-to-all-done.3 = bf16[8,2,55296]{2,1,0:T(2,128)(2,1)S(1)} async-done(((bf16[8,2,55296]{2,1,0:T(2,128)(2,1)}), bf16[8,2,55296]{2,1,0:T(2,128)(2,1)S(1)}, u32[]{:S(2)}, u32[]{:S(2)}) %all-to-all-start.3) | async-done | bytes 1769504 | tf_op jit(solution)/shard_map/all_to_all | solution.py:251
  392.2 6.8 reshape.484
  399.0 6.9 copy.151
  406.0 6.6 multiply_reduce_fusion.2
  457.0 22.1 %collective-permute-done.5 = bf16[256,432]{0,1:T(8,128)(2,1)S(1)} collective-permute-done((bf16[256,432]{0,1:T(8,128)(2,1)S(1)}, bf16[256,432]{0,1:T(8,128)(2,1)S(1)}, u32[]{:S(2)}, u32[]{:S(2)}) %collective-permute-start.5) | collective-permute-done | bytes 221216 | tf_op jit(solution)/shard_map/ppermute | solution.py:142
  486.3 7.0 fusion.53
  505.2 7.2 collective-permute-done.20
  512.4 6.2 collective-permute-done.21
  525.0 8.0 fusion.48
  546.8 5.4 fusion.60
  555.5 13.3 %collective-permute-start.13 = (bf16[256,576]{0,1:T(8,128)(2,1)S(1)}, bf16[256,576]{0,1:T(8,128)(2,1)S(1)}, u32[]{:S(2)}, u32[]{:S(2)}) collective-permute-start(bf16[256,576]{0,1:T(8,128)(2,1)S(1)} %get-tuple-element.324), channel_id=1, source_target_pairs={{0,4},{4,8},{8,12},{12,16},{16,20},{20,24},{24,28},{28,0},{1,5},{5... | collective-permute-start | bytes 884744 | tf_op jit(solution)/shard_map/ppermute | solution.py:142
  568.8 37.8 %collective-permute-start.14 = (bf16[256,576]{0,1:T(8,128)(2,1)S(1)}, bf16[256,576]{0,1:T(8,128)(2,1)S(1)}, u32[]{:S(2)}, u32[]{:S(2)}) collective-permute-start(bf16[256,576]{0,1:T(8,128)(2,1)S(1)} %get-tuple-element.323), channel_id=1, source_target_pairs={{0,8},{4,12},{8,16},{12,20},{16,24},{20,28},{24,0},{28,4},{1,9},{5... | collective-permute-start | bytes 884744 | tf_op jit(solution)/shard_map/ppermute | solution.py:142
  607.4 9.8 %collective-permute-start.15 = (bf16[256,576]{0,1:T(8,128)(2,1)S(1)}, bf16[256,576]{0,1:T(8,128)(2,1)S(1)}, u32[]{:S(2)}, u32[]{:S(2)}) collective-permute-start(bf16[256,576]{0,1:T(8,128)(2,1)S(1)} %get-tuple-element.322), channel_id=1, source_target_pairs={{0,12},{4,16},{8,20},{12,24},{16,28},{20,0},{24,4},{28,8},{1,13},{... | collective-permute-start | bytes 884744 | tf_op jit(solution)/shard_map/ppermute | solution.py:142
  623.0 9.8 %collective-permute-start.19 = (bf16[256,576]{0,1:T(8,128)(2,1)S(1)}, bf16[256,576]{0,1:T(8,128)(2,1)S(1)}, u32[]{:S(2)}, u32[]{:S(2)}) collective-permute-start(bf16[256,576]{0,1:T(8,128)(2,1)S(1)} %get-tuple-element.318), channel_id=1, source_target_pairs={{0,28},{4,0},{8,4},{12,8},{16,12},{20,16},{24,20},{28,24},{1,29},{... | collective-permute-start | bytes 884744 | tf_op jit(solution)/shard_map/ppermute | solution.py:142
  634.2 17.3 %collective-permute-done.16 = bf16[256,576]{0,1:T(8,128)(2,1)S(1)} collective-permute-done((bf16[256,576]{0,1:T(8,128)(2,1)S(1)}, bf16[256,576]{0,1:T(8,128)(2,1)S(1)}, u32[]{:S(2)}, u32[]{:S(2)}) %collective-permute-start.16) | collective-permute-done | bytes 294944 | tf_op jit(solution)/shard_map/ppermute | solution.py:142
  655.5 11.4 %collective-permute-done.18 = bf16[256,576]{0,1:T(8,128)(2,1)S(1)} collective-permute-done((bf16[256,576]{0,1:T(8,128)(2,1)S(1)}, bf16[256,576]{0,1:T(8,128)(2,1)S(1)}, u32[]{:S(2)}, u32[]{:S(2)}) %collective-permute-start.18) | collective-permute-done | bytes 294944 | tf_op jit(solution)/shard_map/ppermute | solution.py:142
  667.7 10.9 %collective-permute-done.19 = bf16[256,576]{0,1:T(8,128)(2,1)S(1)} collective-permute-done((bf16[256,576]{0,1:T(8,128)(2,1)S(1)}, bf16[256,576]{0,1:T(8,128)(2,1)S(1)}, u32[]{:S(2)}, u32[]{:S(2)}) %collective-permute-start.19) | collective-permute-done | bytes 294944 | tf_op jit(solution)/shard_map/ppermute | solution.py:142
  683.5 8.6 %fusion.50 = f32[1152,576]{1,0:T(8,128)} fusion(bf16[2048,1152]{1,0:T(8,128)(2,1)} %all-gather.13.cloned.1.call-done, bf16[2048,576]{0,1:T(8,128)(2,1)} %bitcast.307, pred[2048]{0:T(1024)(128)(4,1)S(1)} %broadcast_in_dim.155), kind=kOutput, calls=%fused_computation.87 | convolution fusion | flops 2719088640 | bytes 9734144 | tf_op jit(solution)/shard_map/dot_general | solution.py:16
  693.4 8.9 %fusion.47 = bf16[1,256,1152]{2,1,0:T(8,128)(2,1)} fusion(f32[256,1152]{1,0:T(8,128)S(1)} %copy-done.8, bf16[256,4608]{1,0:T(8,128)(2,1)} %get-tuple-element.308, bf16[4608,1152]{1,0:T(8,128)(2,1)} %param.35, f32[1152]{0:T(1024)S(1)} %convert_element_type.106), kind=kOutput, calls=%fused_computation.82 | convolution fusion | flops 2718793728 | bytes 14750208 | tf_op jit(solution)/shard_map/dot_general | solution.py:12
  702.5 64.8 %psum.7 = f32[12672]{0:T(1024)S(1)} all-reduce(f32[12672]{0:T(1024)S(1)} %constant_dynamic-update-slice_fusion.1), channel_id=1, replica_groups=mesh['seq'=8,'batch'=4] {'seq','batch'}, use_global_device_ids=true, to_apply=%region_26.27 | all-reduce | flops 12672 | bytes 101376 | tf_op jit(solution)/shard_map/psum | solution.py:285
  774.8 31.7 %reduce-scatter.12.cloned.1.call-done = f32[288,576]{1,0:T(8,128)} async-done(((f32[1152,576]{1,0:T(8,128)}), f32[288,576]{1,0:T(8,128)}) %reduce-scatter.12.cloned.1.call-update) | async-done | bytes 663568 | tf_op jit(solution)/shard_map/reduce_scatter | solution.py:158
  (361 shorter events, 319.3 us)
Async XLA Ops:
  28.5 48.9 %all-to-all-start = ((bf16[256,3,8,144]{0,3,1,2:T(8,128)(2,1)}), bf16[256,3,8,144]{0,3,1,2:T(8,128)(2,1)}, u32[]{:S(2)}, u32[]{:S(2)}) async-start(bf16[256,3,8,144]{0,3,1,2:T(8,128)(2,1)} %copy.125), calls=%async_computation | async-start | bytes 3538944 | tf_op jit(solution)/shard_map/all_to_all | solution.py:207
  135.8 20.9 %all-to-all-start.1 = ((bf16[8,256,144]{1,2,0:T(8,128)(2,1)}), bf16[8,256,144]{1,2,0:T(8,128)(2,1)}, u32[]{:S(2)}, u32[]{:S(2)}) async-start(bf16[8,256,144]{1,2,0:T(8,128)(2,1)} %copy.129), calls=%async_computation.1 | async-start | bytes 1179648 | tf_op jit(solution)/shard_map/all_to_all | solution.py:219
  140.0 290.8 %all-gather.11.cloned.1.call-start = ((), (), s32[]{:S(2)}) async-start(), calls=%async_computation.13 | async-start | bytes 2949120 | tf_op jit(solution)/shard_map/all_gather | solution.py:163
  210.1 20.2 %all-to-all-start.2 = ((bf16[256,8,144]{0,2,1:T(8,128)(2,1)}), bf16[256,8,144]{0,2,1:T(8,128)(2,1)S(1)}, u32[]{:S(2)}, u32[]{:S(2)}) async-start(bf16[256,8,144]{0,2,1:T(8,128)(2,1)} %bitcast.18), calls=%async_computation.2 | async-start | bytes 1179648 | tf_op jit(solution)/shard_map/all_to_all | solution.py:245
  213.7 272.6 %all-gather.9.cloned.1.call-start = ((), (), s32[]{:S(2)}) async-start(), calls=%async_computation.11 | async-start | bytes 5308416 | tf_op jit(solution)/shard_map/all_gather | solution.py:155
  346.4 45.7 %all-to-all-start.3 = ((bf16[8,2,55296]{2,1,0:T(2,128)(2,1)}), bf16[8,2,55296]{2,1,0:T(2,128)(2,1)S(1)}, u32[]{:S(2)}, u32[]{:S(2)}) async-start(bf16[8,2,55296]{2,1,0:T(2,128)(2,1)} %reshape.483), calls=%async_computation.3 | async-start | bytes 3538944 | tf_op jit(solution)/shard_map/all_to_all | solution.py:251
  350.3 174.7 %all-gather.15.cloned.1.call-start = ((), (), s32[]{:S(2)}) async-start(), calls=%async_computation.18 | async-start | bytes 2949120 | tf_op jit(solution)/shard_map/all_gather | solution.py:163
  351.0 195.8 %all-gather.7.cloned.1.call-start = ((), (), s32[]{:S(2)}) async-start(), calls=%async_computation.9 | async-start | bytes 2949120 | tf_op jit(solution)/shard_map/all_gather | solution.py:163
  415.2 268.3 %all-gather.13.cloned.1.call-start = ((), (), s32[]{:S(2)}) async-start(), calls=%async_computation.15 | async-start | bytes 5308416 | tf_op jit(solution)/shard_map/all_gather | solution.py:155
  415.8 359.0 %reduce-scatter.10.cloned.1.call-start = ((), (), s32[]{:S(2)}) async-start(), calls=%async_computation.14 | async-start | bytes 1990656 | tf_op jit(solution)/shard_map/reduce_scatter | solution.py:165
  418.6 9.8 %collective-permute-start.11 = (bf16[256,288]{0,1:T(8,128)(2,1)S(1)}, bf16[256,288]{0,1:T(8,128)(2,1)S(1)}, u32[]{:S(2)}, u32[]{:S(2)}) collective-permute-start(bf16[256,288]{0,1:T(8,128)(2,1)S(1)} %get-tuple-element.343), channel_id=1, source_target_pairs={{0,2},{1,3},{2,0},{3,1},{4,6},{5,7},{6,4},{7,5},{8,10},{9,11},{10,... | collective-permute-start | bytes 442376 | tf_op jit(solution)/shard_map/ppermute | solution.py:142
  420.1 9.9 %collective-permute-start.12 = (bf16[256,288]{0,1:T(8,128)(2,1)S(1)}, bf16[256,288]{0,1:T(8,128)(2,1)S(1)}, u32[]{:S(2)}, u32[]{:S(2)}) collective-permute-start(bf16[256,288]{0,1:T(8,128)(2,1)S(1)} %get-tuple-element.342), channel_id=1, source_target_pairs={{0,3},{1,0},{2,1},{3,2},{4,7},{5,4},{6,5},{7,6},{8,11},{9,8},{10,9... | collective-permute-start | bytes 442376 | tf_op jit(solution)/shard_map/ppermute | solution.py:142
  435.3 339.6 %reduce-scatter.8.cloned.1.call-start = ((), (), s32[]{:S(2)}) async-start(), calls=%async_computation.12 | async-start | bytes 2949120 | tf_op jit(solution)/shard_map/reduce_scatter | solution.py:158
  442.7 10.3 %collective-permute-start.4 = (bf16[256,432]{0,1:T(8,128)(2,1)S(1)}, bf16[256,432]{0,1:T(8,128)(2,1)S(1)}, u32[]{:S(2)}, u32[]{:S(2)}) collective-permute-start(bf16[256,432]{0,1:T(8,128)(2,1)S(1)} %get-tuple-element.332), channel_id=1, source_target_pairs={{0,8},{4,12},{8,16},{12,20},{16,24},{20,28},{24,0},{28,4},{1,9},{5... | collective-permute-start | bytes 663560 | tf_op jit(solution)/shard_map/ppermute | solution.py:142
  442.7 36.4 %collective-permute-start.5 = (bf16[256,432]{0,1:T(8,128)(2,1)S(1)}, bf16[256,432]{0,1:T(8,128)(2,1)S(1)}, u32[]{:S(2)}, u32[]{:S(2)}) collective-permute-start(bf16[256,432]{0,1:T(8,128)(2,1)S(1)} %get-tuple-element.331), channel_id=1, source_target_pairs={{0,12},{4,16},{8,20},{12,24},{16,28},{20,0},{24,4},{28,8},{1,13},{... | collective-permute-start | bytes 663560 | tf_op jit(solution)/shard_map/ppermute | solution.py:142
  443.1 36.8 %collective-permute-start.6 = (bf16[256,432]{0,1:T(8,128)(2,1)S(1)}, bf16[256,432]{0,1:T(8,128)(2,1)S(1)}, u32[]{:S(2)}, u32[]{:S(2)}) collective-permute-start(bf16[256,432]{0,1:T(8,128)(2,1)S(1)} %get-tuple-element.330), channel_id=1, source_target_pairs={{0,16},{4,20},{8,24},{12,28},{16,0},{20,4},{24,8},{28,12},{1,17},{... | collective-permute-start | bytes 663560 | tf_op jit(solution)/shard_map/ppermute | solution.py:142
  446.8 33.7 %collective-permute-start.7 = (bf16[256,432]{0,1:T(8,128)(2,1)S(1)}, bf16[256,432]{0,1:T(8,128)(2,1)S(1)}, u32[]{:S(2)}, u32[]{:S(2)}) collective-permute-start(bf16[256,432]{0,1:T(8,128)(2,1)S(1)} %get-tuple-element.329), channel_id=1, source_target_pairs={{0,20},{4,24},{8,28},{12,0},{16,4},{20,8},{24,12},{28,16},{1,21},{... | collective-permute-start | bytes 663560 | tf_op jit(solution)/shard_map/ppermute | solution.py:142
  451.7 29.5 %collective-permute-start.8 = (bf16[256,432]{0,1:T(8,128)(2,1)S(1)}, bf16[256,432]{0,1:T(8,128)(2,1)S(1)}, u32[]{:S(2)}, u32[]{:S(2)}) collective-permute-start(bf16[256,432]{0,1:T(8,128)(2,1)S(1)} %get-tuple-element.328), channel_id=1, source_target_pairs={{0,24},{4,28},{8,0},{12,4},{16,8},{20,12},{24,16},{28,20},{1,25},{... | collective-permute-start | bytes 663560 | tf_op jit(solution)/shard_map/ppermute | solution.py:142
  453.0 28.9 %collective-permute-start.9 = (bf16[256,432]{0,1:T(8,128)(2,1)S(1)}, bf16[256,432]{0,1:T(8,128)(2,1)S(1)}, u32[]{:S(2)}, u32[]{:S(2)}) collective-permute-start(bf16[256,432]{0,1:T(8,128)(2,1)S(1)} %get-tuple-element.327), channel_id=1, source_target_pairs={{0,28},{4,0},{8,4},{12,8},{16,12},{20,16},{24,20},{28,24},{1,29},{... | collective-permute-start | bytes 663560 | tf_op jit(solution)/shard_map/ppermute | solution.py:142
  493.3 281.5 %reduce-scatter.14.cloned.1.call-start = ((), (), s32[]{:S(2)}) async-start(), calls=%async_computation.17 | async-start | bytes 5971968 | tf_op jit(solution)/shard_map/reduce_scatter | solution.py:165
  501.4 10.9 %collective-permute-start.20 = (bf16[256,1152]{1,0:T(8,128)(2,1)S(1)}, bf16[256,1152]{1,0:T(8,128)(2,1)S(1)}, u32[]{:S(2)}, u32[]{:S(2)}) collective-permute-start(bf16[256,1152]{1,0:T(8,128)(2,1)S(1)} %bitcast.317), channel_id=1, source_target_pairs={{0,1},{1,2},{2,3},{3,0},{4,5},{5,6},{6,7},{7,4},{8,9},{9,10},{10,1... | collective-permute-start | bytes 1769480 | tf_op jit(solution)/shard_map/ppermute | solution.py:142
  503.1 15.5 %collective-permute-start.21 = (bf16[256,1152]{1,0:T(8,128)(2,1)S(1)}, bf16[256,1152]{1,0:T(8,128)(2,1)S(1)}, u32[]{:S(2)}, u32[]{:S(2)}) collective-permute-start(bf16[256,1152]{1,0:T(8,128)(2,1)S(1)} %bitcast.318), channel_id=1, source_target_pairs={{0,2},{1,3},{2,0},{3,1},{4,6},{5,7},{6,4},{7,5},{8,10},{9,11},{10,... | collective-permute-start | bytes 1769480 | tf_op jit(solution)/shard_map/ppermute | solution.py:142
  503.3 15.3 %collective-permute-start.22 = (bf16[256,1152]{1,0:T(8,128)(2,1)S(1)}, bf16[256,1152]{1,0:T(8,128)(2,1)S(1)}, u32[]{:S(2)}, u32[]{:S(2)}) collective-permute-start(bf16[256,1152]{1,0:T(8,128)(2,1)S(1)} %bitcast.319), channel_id=1, source_target_pairs={{0,3},{1,0},{2,1},{3,2},{4,7},{5,4},{6,5},{7,6},{8,11},{9,8},{10,9... | collective-permute-start | bytes 1769480 | tf_op jit(solution)/shard_map/ppermute | solution.py:142
  533.0 241.8 %reduce-scatter.6.cloned.1.call-start = ((), (), s32[]{:S(2)}) async-start(), calls=%async_computation.10 | async-start | bytes 3317760 | tf_op jit(solution)/shard_map/reduce_scatter | solution.py:165
  552.3 254.2 %reduce-scatter.12.cloned.1.call-start = ((), (), s32[]{:S(2)}) async-start(), calls=%async_computation.16 | async-start | bytes 3686400 | tf_op jit(solution)/shard_map/reduce_scatter | solution.py:158
  555.5 64.0 %collective-permute-start.13 = (bf16[256,576]{0,1:T(8,128)(2,1)S(1)}, bf16[256,576]{0,1:T(8,128)(2,1)S(1)}, u32[]{:S(2)}, u32[]{:S(2)}) collective-permute-start(bf16[256,576]{0,1:T(8,128)(2,1)S(1)} %get-tuple-element.324), channel_id=1, source_target_pairs={{0,4},{4,8},{8,12},{12,16},{16,20},{20,24},{24,28},{28,0},{1,5},{5... | collective-permute-start | bytes 884744 | tf_op jit(solution)/shard_map/ppermute | solution.py:142
  568.8 54.2 %collective-permute-start.14 = (bf16[256,576]{0,1:T(8,128)(2,1)S(1)}, bf16[256,576]{0,1:T(8,128)(2,1)S(1)}, u32[]{:S(2)}, u32[]{:S(2)}) collective-permute-start(bf16[256,576]{0,1:T(8,128)(2,1)S(1)} %get-tuple-element.323), channel_id=1, source_target_pairs={{0,8},{4,12},{8,16},{12,20},{16,24},{20,28},{24,0},{28,4},{1,9},{5... | collective-permute-start | bytes 884744 | tf_op jit(solution)/shard_map/ppermute | solution.py:142
  607.4 26.1 %collective-permute-start.15 = (bf16[256,576]{0,1:T(8,128)(2,1)S(1)}, bf16[256,576]{0,1:T(8,128)(2,1)S(1)}, u32[]{:S(2)}, u32[]{:S(2)}) collective-permute-start(bf16[256,576]{0,1:T(8,128)(2,1)S(1)} %get-tuple-element.322), channel_id=1, source_target_pairs={{0,12},{4,16},{8,20},{12,24},{16,28},{20,0},{24,4},{28,8},{1,13},{... | collective-permute-start | bytes 884744 | tf_op jit(solution)/shard_map/ppermute | solution.py:142
  617.2 34.4 %collective-permute-start.16 = (bf16[256,576]{0,1:T(8,128)(2,1)S(1)}, bf16[256,576]{0,1:T(8,128)(2,1)S(1)}, u32[]{:S(2)}, u32[]{:S(2)}) collective-permute-start(bf16[256,576]{0,1:T(8,128)(2,1)S(1)} %get-tuple-element.321), channel_id=1, source_target_pairs={{0,16},{4,20},{8,24},{12,28},{16,0},{20,4},{24,8},{28,12},{1,17},{... | collective-permute-start | bytes 884744 | tf_op jit(solution)/shard_map/ppermute | solution.py:142
  617.2 37.6 %collective-permute-start.17 = (bf16[256,576]{0,1:T(8,128)(2,1)S(1)}, bf16[256,576]{0,1:T(8,128)(2,1)S(1)}, u32[]{:S(2)}, u32[]{:S(2)}) collective-permute-start(bf16[256,576]{0,1:T(8,128)(2,1)S(1)} %get-tuple-element.320), channel_id=1, source_target_pairs={{0,20},{4,24},{8,28},{12,0},{16,4},{20,8},{24,12},{28,16},{1,21},{... | collective-permute-start | bytes 884744 | tf_op jit(solution)/shard_map/ppermute | solution.py:142
  619.5 47.4 %collective-permute-start.18 = (bf16[256,576]{0,1:T(8,128)(2,1)S(1)}, bf16[256,576]{0,1:T(8,128)(2,1)S(1)}, u32[]{:S(2)}, u32[]{:S(2)}) collective-permute-start(bf16[256,576]{0,1:T(8,128)(2,1)S(1)} %get-tuple-element.319), channel_id=1, source_target_pairs={{0,24},{4,28},{8,0},{12,4},{16,8},{20,12},{24,16},{28,20},{1,25},{... | collective-permute-start | bytes 884744 | tf_op jit(solution)/shard_map/ppermute | solution.py:142
  623.0 55.6 %collective-permute-start.19 = (bf16[256,576]{0,1:T(8,128)(2,1)S(1)}, bf16[256,576]{0,1:T(8,128)(2,1)S(1)}, u32[]{:S(2)}, u32[]{:S(2)}) collective-permute-start(bf16[256,576]{0,1:T(8,128)(2,1)S(1)} %get-tuple-element.318), channel_id=1, source_target_pairs={{0,28},{4,0},{8,4},{12,8},{16,12},{20,16},{24,20},{28,24},{1,29},{... | collective-permute-start | bytes 884744 | tf_op jit(solution)/shard_map/ppermute | solution.py:142
  (56 other events, 564.9 us)
Sparse Core Ops, SparseCore 0:
  205.2 36.2 all-gather.10
  243.1 51.1 all-gather.8
  352.9 38.6 all-gather.14
  415.3 36.7 all-gather.6
  453.6 71.3 all-gather.12
  527.7 32.4 reduce-scatter.9
  563.9 43.4 reduce-scatter.7
  610.2 103.6 reduce-scatter.13
  716.8 44.0 reduce-scatter.5
  764.4 42.0 reduce-scatter.11
where the time goes:
time: 820 us; the launch traced here: 814 us
  waiting for transfers between devices  246 us (30%)
  matrix products  208 us (25%)
  local copies, waits for them, and re-layouts  120 us (15%)
  starting transfers between devices  115 us (14%)
  blocking collectives  64.8 us (8%)
  other arithmetic  43.7 us (5%)
  between operations  15.3 us (2%)
    ppermute x23, waiting for transfers between devices, exchange(): got.append(lax.ppermute(piece, axis, pairs))  97.9 us
    ppermute x23, starting transfers between devices, exchange(): got.append(lax.ppermute(piece, axis, pairs))  94.7 us
    psum x1, blocking collectives, on_device(): small_total = lax.psum(jnp.concatenate(small_grads), ('seq', 'batch'))  64.8 us
    all_to_all x1, waiting for transfers between devices, on_device(): lax.all_to_all(packed.reshape(local_rows, 3, seq_count, feature_count //...  41.7 us
    all_to_all x1, waiting for transfers between devices, on_device(): lax.all_to_all(jnp.stack([grad_query, grad_key, grad_value], axis=1)[:, :...  41.1 us
    dot_general x5, matrix products, product(): return jnp.dot(left, right, preferred_element_type=jnp.float32)  40.5 us
    dot_general x5, matrix products, times_transposed(): lax.dot_general(left, right, (((1,), (1,)), ((), ())), preferred_element_...  37.6 us
    unnamed x100, local copies, waits for them, and re-layouts  33.6 us
  transfers between devices with their start and end apart: 37, of which 19 were waited for; matrix products, arithmetic and copies ran while one was open for 30% of the time, Pallas kernels for 0%

commit v1 on v0

--- a/solution.py
+++ b/solution.py
@@ -282,7 +282,8 @@
         grad_down_bias,
     )
     small_sizes = [piece.shape[0] for piece in small_grads]
-    small_total = lax.psum(jnp.concatenate(small_grads), ("seq", "batch"))
+    lay_the_wires = lambda arr: lax.all_gather(arr, ("seq", "batch")).sum(axis=0)
+    small_total = lay_the_wires(jnp.concatenate(small_grads))
     summed_small = []
     offset = 0
     for size in small_sizes:

time: 820 us -> 826 us (level)
  waiting for transfers between devices: 246 us -> 320 us
  blocking collectives: 64.8 us -> 0 us
    reduce_scatter x3, waiting for transfers between devices: 0.02 us -> 85.5 us  [batch_gathered_grad(): return lax.psum_scatter(partial, 'seq', scatter_dimension=1, tiled=True)]
    psum x1 -> x0, blocking collectives: 64.8 us -> none  [on_device(): small_total = lax.psum(jnp.concatenate(small_grads), ('seq', 'batch'))]
    ppermute x23, waiting for transfers between devices: 97.9 us -> 71.9 us  [exchange(): got.append(lax.ppermute(piece, axis, pairs))]
    reduce_scatter x2, waiting for transfers between devices: 31.7 us -> 45.5 us  [seq_gathered_grad(): return lax.psum_scatter(partial, 'batch', scatter_dimension=0, tiled=True)]
    unnamed x100 -> x93, local copies, waits for them, and re-layouts: 33.6 us -> 34.2 us
  transfers between devices with their start and end apart: 37 -> 38, of which waited for: 19 -> 20; matrix products, arithmetic and copies ran while one was open for 30% -> 30% of each run, Pallas kernels for 0% -> 0%
where the time goes in v1:
time: 826 us; the launch traced here: 820 us
  waiting for transfers between devices  320 us (39%)
  matrix products  207 us (25%)
  local copies, waits for them, and re-layouts  121 us (15%)
  starting transfers between devices  112 us (14%)
  other arithmetic  45.4 us (5%)
  between operations  15 us (2%)
    ppermute x23, starting transfers between devices, exchange(): got.append(lax.ppermute(piece, axis, pairs))  92 us
    reduce_scatter x3, waiting for transfers between devices, batch_gathered_grad(): return lax.psum_scatter(partial, 'seq', scatter_dimension=1, tiled=True)  85.5 us
    ppermute x23, waiting for transfers between devices, exchange(): got.append(lax.ppermute(piece, axis, pairs))  71.9 us
    reduce_scatter x2, waiting for transfers between devices, seq_gathered_grad(): return lax.psum_scatter(partial, 'batch', scatter_dimension=0, tiled=True)  45.5 us
    all_to_all x1, waiting for transfers between devices, on_device(): lax.all_to_all(packed.reshape(local_rows, 3, seq_count, feature_count //...  41.7 us
    all_to_all x1, waiting for transfers between devices, on_device(): lax.all_to_all(jnp.stack([grad_query, grad_key, grad_value], axis=1)[:, :...  41.1 us
    dot_general x5, matrix products, product(): return jnp.dot(left, right, preferred_element_type=jnp.float32)  40.5 us
    dot_general x5, matrix products, times_transposed(): lax.dot_general(left, right, (((1,), (1,)), ((), ())), preferred_element_...  36.1 us
  transfers between devices with their start and end apart: 38, of which 20 were waited for; matrix products, arithmetic and copies ran while one was open for 30% of the time, Pallas kernels for 0%

profile of v1, /device:TPU:0, one launch (start us, length us, event | category | flops | bytes accessed | tf_op | source)
XLA Modules:
  0.0 820.1 jit_solution(1159621269381390586)
XLA Ops:
  14.6 7.2 convolution_convert_fusion
  28.4 6.8 all-to-all-start
  35.6 41.7 %all-to-all-done = bf16[256,3,8,144]{0,3,1,2:T(8,128)(2,1)} async-done(((bf16[256,3,8,144]{0,3,1,2:T(8,128)(2,1)}), bf16[256,3,8,144]{0,3,1,2:T(8,128)(2,1)}, u32[]{:S(2)}, u32[]{:S(2)}) %all-to-all-start) | async-done | bytes 1769504 | tf_op jit(solution)/shard_map/all_to_all | solution.py:207
  92.6 36.5 %while.27 = (s32[]{:T(128)}, bf16[4,512,144]{1,2,0:T(8,128)(2,1)}, f32[4,2,512,1]{2,1,3,0:T(2,128)S(1)}, s32[4,512]{1,0:T(4,128)S(1)}, s32[2048]{0:T(1024)S(1)},...) while((s32[]{:T(128)}, bf16[4,512,144]{1,2,0:T(8,128)(2,1)}, ...), condition=%wide.region_7.8_spmd, body=%wide.region_4.7_spmd.sunk | while | flops 628169728 | bytes 33537152 | solution.py:74
  140.6 16.1 %all-to-all-done.1 = bf16[8,256,144]{1,2,0:T(8,128)(2,1)} async-done(((bf16[8,256,144]{1,2,0:T(8,128)(2,1)}), bf16[8,256,144]{1,2,0:T(8,128)(2,1)}, u32[]{:S(2)}, u32[]{:S(2)}) %all-to-all-start.1) | async-done | bytes 589856 | tf_op jit(solution)/shard_map/all_to_all | solution.py:219
  161.4 17.2 %multiply_convert_fusion.1 = (bf16[256,4608]{1,0:T(8,128)(2,1)}, f32[256,4608]{1,0:T(8,128)}, f32[256,4608]{1,0:T(8,128)}) fusion(f32[4608]{0:T(1024)S(1)} %convert_element_type.104, bf16[256,1152]{1,0:T(8,128)(2,1)} %add_convert_fusion.2, bf16[1152,4608]{1,0:T(8,128)(2,1)} %param.33), kind=kOutput, calls=%fused_computation.61 | convolution fusion | flops 2795765760 | bytes 23021568 | tf_op jit(solution)/shard_map/dot_general | solution.py:12
  178.6 14.0 %convert_reduce_fusion = (f32[4608]{0:T(1024)S(1)}, bf16[256,4608]{1,0:T(8,128)(2,1)}) fusion(f32[256,4608]{1,0:T(8,128)} %get-tuple-element.309, f32[256,4608]{1,0:T(8,128)} %get-tuple-element.357, bf16[4608,1152]{1,0:T(8,128)(2,1)} %param.35, bf16[1,256,1152]{2,1,0:T(8,128)(2,1)S(1)} %copy-done.13), kind=kOutput, calls=%fused_computation.59 | convolution fusion | flops 2736778752 | bytes 23021568 | tf_op jit(solution)/shard_map/dot_general | solution.py:22
  192.6 8.1 multiply_reduce_fusion.1
  212.7 15.9 %all-to-all-done.2 = bf16[256,8,144]{0,2,1:T(8,128)(2,1)S(1)} async-done(((bf16[256,8,144]{0,2,1:T(8,128)(2,1)}), bf16[256,8,144]{0,2,1:T(8,128)(2,1)S(1)}, u32[]{:S(2)}, u32[]{:S(2)}) %all-to-all-start.2) | async-done | bytes 589856 | tf_op jit(solution)/shard_map/all_to_all | solution.py:245
  231.0 96.8 %while.28 = (s32[]{:T(128)}, f32[2048,2,72]{0,2,1:T(8,128)S(1)}, f32[2048,2,72]{0,2,1:T(8,128)}, bf16[4,512,144]{1,2,0:T(8,128)(2,1)}, bf16[4,512,2,72]{1,3,2,0:...) while((s32[]{:T(128)}, f32[2048,2,72]{0,2,1:T(8,128)S(1)}, ...), condition=%wide.region_14.15_spmd.clone, body=%wide.region_12.14_spmd.clone.sunk | while | flops 1543781376 | bytes 144143088 | solution.py:120
  336.1 8.6 %reshape.487 = bf16[8,2,55296]{2,1,0:T(2,128)(2,1)} reshape(bf16[2048,1,3,144]{3,2,1,0:T(4,128)(2,1)} %bitcast.291) | data formatting | bytes 3538944
  349.2 41.1 %all-to-all-done.3 = bf16[8,2,55296]{2,1,0:T(2,128)(2,1)S(1)} async-done(((bf16[8,2,55296]{2,1,0:T(2,128)(2,1)}), bf16[8,2,55296]{2,1,0:T(2,128)(2,1)S(1)}, u32[]{:S(2)}, u32[]{:S(2)}) %all-to-all-start.3) | async-done | bytes 1769504 | tf_op jit(solution)/shard_map/all_to_all | solution.py:251
  390.4 6.8 reshape.488
  397.2 6.9 copy.151
  404.1 6.6 multiply_reduce_fusion.2
  435.1 5.4 copy.150
  456.7 23.3 %collective-permute-done.5 = bf16[256,432]{0,1:T(8,128)(2,1)S(1)} collective-permute-done((bf16[256,432]{0,1:T(8,128)(2,1)S(1)}, bf16[256,432]{0,1:T(8,128)(2,1)S(1)}, u32[]{:S(2)}, u32[]{:S(2)}) %collective-permute-start.5) | collective-permute-done | bytes 221216 | tf_op jit(solution)/shard_map/ppermute | solution.py:142
  487.1 7.0 fusion.53
  505.6 7.6 collective-permute-done.20
  513.2 6.2 collective-permute-done.21
  525.7 8.0 fusion.48
  547.4 5.4 fusion.60
  556.1 12.8 %collective-permute-start.13 = (bf16[256,576]{0,1:T(8,128)(2,1)S(1)}, bf16[256,576]{0,1:T(8,128)(2,1)S(1)}, u32[]{:S(2)}, u32[]{:S(2)}) collective-permute-start(bf16[256,576]{0,1:T(8,128)(2,1)S(1)} %get-tuple-element.324), channel_id=1, source_target_pairs={{0,4},{4,8},{8,12},{12,16},{16,20},{20,24},{24,28},{28,0},{1,5},{5... | collective-permute-start | bytes 884744 | tf_op jit(solution)/shard_map/ppermute | solution.py:142
  568.8 34.4 %collective-permute-start.14 = (bf16[256,576]{0,1:T(8,128)(2,1)S(1)}, bf16[256,576]{0,1:T(8,128)(2,1)S(1)}, u32[]{:S(2)}, u32[]{:S(2)}) collective-permute-start(bf16[256,576]{0,1:T(8,128)(2,1)S(1)} %get-tuple-element.323), channel_id=1, source_target_pairs={{0,8},{4,12},{8,16},{12,20},{16,24},{20,28},{24,0},{28,4},{1,9},{5... | collective-permute-start | bytes 884744 | tf_op jit(solution)/shard_map/ppermute | solution.py:142
  604.0 11.4 %collective-permute-start.15 = (bf16[256,576]{0,1:T(8,128)(2,1)S(1)}, bf16[256,576]{0,1:T(8,128)(2,1)S(1)}, u32[]{:S(2)}, u32[]{:S(2)}) collective-permute-start(bf16[256,576]{0,1:T(8,128)(2,1)S(1)} %get-tuple-element.322), channel_id=1, source_target_pairs={{0,12},{4,16},{8,20},{12,24},{16,28},{20,0},{24,4},{28,8},{1,13},{... | collective-permute-start | bytes 884744 | tf_op jit(solution)/shard_map/ppermute | solution.py:142
  617.8 7.7 collective-permute-start.18
  635.8 6.6 collective-permute-done.16
  653.7 8.9 %fusion.50 = f32[1152,576]{1,0:T(8,128)} fusion(bf16[2048,1152]{1,0:T(8,128)(2,1)} %all-gather.16.cloned.1.call-done, bf16[2048,576]{0,1:T(8,128)(2,1)} %bitcast.307, pred[2048]{0:T(1024)(128)(4,1)S(1)} %broadcast_in_dim.155), kind=kOutput, calls=%fused_computation.87 | convolution fusion | flops 2719088640 | bytes 9734144 | tf_op jit(solution)/shard_map/dot_general | solution.py:16
  663.9 8.8 %fusion.47 = bf16[1,256,1152]{2,1,0:T(8,128)(2,1)} fusion(f32[256,1152]{1,0:T(8,128)S(1)} %copy-done.8, bf16[256,4608]{1,0:T(8,128)(2,1)} %get-tuple-element.308, bf16[4608,1152]{1,0:T(8,128)(2,1)} %param.35, f32[1152]{0:T(1024)S(1)} %convert_element_type.106), kind=kOutput, calls=%fused_computation.82 | convolution fusion | flops 2718793728 | bytes 14750208 | tf_op jit(solution)/shard_map/dot_general | solution.py:12
  682.4 45.1 %reduce-scatter.14.cloned.1.call-done = f32[1152,144]{0,1:T(8,128)} async-done(((f32[1152,1152]{0,1:T(8,128)}), f32[1152,144]{0,1:T(8,128)}) %reduce-scatter.14.cloned.1.call-update) | async-done | bytes 663568 | tf_op jit(solution)/shard_map/reduce_scatter | solution.py:165
  727.5 40.4 %reduce-scatter.6.cloned.1.call-done = f32[576,144]{0,1:T(8,128)} async-done(((f32[576,1152]{0,1:T(8,128)}), f32[576,144]{0,1:T(8,128)}) %reduce-scatter.6.cloned.1.call-update) | async-done | bytes 331792 | tf_op jit(solution)/shard_map/reduce_scatter | solution.py:165
  767.9 45.4 %reduce-scatter.12.cloned.1.call-done = f32[288,576]{1,0:T(8,128)} async-done(((f32[1152,576]{1,0:T(8,128)}), f32[288,576]{1,0:T(8,128)}) %reduce-scatter.12.cloned.1.call-update) | async-done | bytes 663568 | tf_op jit(solution)/shard_map/reduce_scatter | solution.py:158
  (357 shorter events, 323.1 us)
Async XLA Ops:
  28.4 48.9 %all-to-all-start = ((bf16[256,3,8,144]{0,3,1,2:T(8,128)(2,1)}), bf16[256,3,8,144]{0,3,1,2:T(8,128)(2,1)}, u32[]{:S(2)}, u32[]{:S(2)}) async-start(bf16[256,3,8,144]{0,3,1,2:T(8,128)(2,1)} %copy.125), calls=%async_computation | async-start | bytes 3538944 | tf_op jit(solution)/shard_map/all_to_all | solution.py:207
  135.7 20.9 %all-to-all-start.1 = ((bf16[8,256,144]{1,2,0:T(8,128)(2,1)}), bf16[8,256,144]{1,2,0:T(8,128)(2,1)}, u32[]{:S(2)}, u32[]{:S(2)}) async-start(bf16[8,256,144]{1,2,0:T(8,128)(2,1)} %copy.129), calls=%async_computation.1 | async-start | bytes 1179648 | tf_op jit(solution)/shard_map/all_to_all | solution.py:219
  139.9 290.7 %all-gather.14.cloned.1.call-start = ((), (), s32[]{:S(2)}) async-start(), calls=%async_computation.13 | async-start | bytes 2949120 | tf_op jit(solution)/shard_map/all_gather | solution.py:163
  208.3 20.2 %all-to-all-start.2 = ((bf16[256,8,144]{0,2,1:T(8,128)(2,1)}), bf16[256,8,144]{0,2,1:T(8,128)(2,1)S(1)}, u32[]{:S(2)}, u32[]{:S(2)}) async-start(bf16[256,8,144]{0,2,1:T(8,128)(2,1)} %bitcast.18), calls=%async_computation.2 | async-start | bytes 1179648 | tf_op jit(solution)/shard_map/all_to_all | solution.py:245
  211.9 275.2 %all-gather.12.cloned.1.call-start = ((), (), s32[]{:S(2)}) async-start(), calls=%async_computation.11 | async-start | bytes 5308416 | tf_op jit(solution)/shard_map/all_gather | solution.py:155
  344.6 45.7 %all-to-all-start.3 = ((bf16[8,2,55296]{2,1,0:T(2,128)(2,1)}), bf16[8,2,55296]{2,1,0:T(2,128)(2,1)S(1)}, u32[]{:S(2)}, u32[]{:S(2)}) async-start(bf16[8,2,55296]{2,1,0:T(2,128)(2,1)} %reshape.487), calls=%async_computation.3 | async-start | bytes 3538944 | tf_op jit(solution)/shard_map/all_to_all | solution.py:251
  348.4 177.3 %all-gather.18.cloned.1.call-start = ((), (), s32[]{:S(2)}) async-start(), calls=%async_computation.18 | async-start | bytes 2949120 | tf_op jit(solution)/shard_map/all_gather | solution.py:163
  349.2 198.2 %all-gather.10.cloned.1.call-start = ((), (), s32[]{:S(2)}) async-start(), calls=%async_computation.9 | async-start | bytes 2949120 | tf_op jit(solution)/shard_map/all_gather | solution.py:163
  413.3 240.4 %all-gather.16.cloned.1.call-start = ((), (), s32[]{:S(2)}) async-start(), calls=%async_computation.15 | async-start | bytes 5308416 | tf_op jit(solution)/shard_map/all_gather | solution.py:155
  413.9 264.9 %all-gather.20.cloned.1.call-start = ((), (), s32[]{:S(2)}) async-start(), calls=%async_computation.19 | async-start | bytes 1672704 | tf_op jit(solution)/shard_map/all_gather | solution.py:285
  414.8 267.6 %reduce-scatter.10.cloned.1.call-start = ((), (), s32[]{:S(2)}) async-start(), calls=%async_computation.14 | async-start | bytes 1990656 | tf_op jit(solution)/shard_map/reduce_scatter | solution.py:165
  419.1 10.7 %collective-permute-start.12 = (bf16[256,288]{0,1:T(8,128)(2,1)S(1)}, bf16[256,288]{0,1:T(8,128)(2,1)S(1)}, u32[]{:S(2)}, u32[]{:S(2)}) collective-permute-start(bf16[256,288]{0,1:T(8,128)(2,1)S(1)} %get-tuple-element.342), channel_id=1, source_target_pairs={{0,3},{1,0},{2,1},{3,2},{4,7},{5,4},{6,5},{7,6},{8,11},{9,8},{10,9... | collective-permute-start | bytes 442376 | tf_op jit(solution)/shard_map/ppermute | solution.py:142
  435.1 247.4 %reduce-scatter.8.cloned.1.call-start = ((), (), s32[]{:S(2)}) async-start(), calls=%async_computation.12 | async-start | bytes 2949120 | tf_op jit(solution)/shard_map/reduce_scatter | solution.py:158
  442.6 10.3 %collective-permute-start.4 = (bf16[256,432]{0,1:T(8,128)(2,1)S(1)}, bf16[256,432]{0,1:T(8,128)(2,1)S(1)}, u32[]{:S(2)}, u32[]{:S(2)}) collective-permute-start(bf16[256,432]{0,1:T(8,128)(2,1)S(1)} %get-tuple-element.332), channel_id=1, source_target_pairs={{0,8},{4,12},{8,16},{12,20},{16,24},{20,28},{24,0},{28,4},{1,9},{5... | collective-permute-start | bytes 663560 | tf_op jit(solution)/shard_map/ppermute | solution.py:142
  442.6 37.3 %collective-permute-start.5 = (bf16[256,432]{0,1:T(8,128)(2,1)S(1)}, bf16[256,432]{0,1:T(8,128)(2,1)S(1)}, u32[]{:S(2)}, u32[]{:S(2)}) collective-permute-start(bf16[256,432]{0,1:T(8,128)(2,1)S(1)} %get-tuple-element.331), channel_id=1, source_target_pairs={{0,12},{4,16},{8,20},{12,24},{16,28},{20,0},{24,4},{28,8},{1,13},{... | collective-permute-start | bytes 663560 | tf_op jit(solution)/shard_map/ppermute | solution.py:142
  442.8 37.8 %collective-permute-start.6 = (bf16[256,432]{0,1:T(8,128)(2,1)S(1)}, bf16[256,432]{0,1:T(8,128)(2,1)S(1)}, u32[]{:S(2)}, u32[]{:S(2)}) collective-permute-start(bf16[256,432]{0,1:T(8,128)(2,1)S(1)} %get-tuple-element.330), channel_id=1, source_target_pairs={{0,16},{4,20},{8,24},{12,28},{16,0},{20,4},{24,8},{28,12},{1,17},{... | collective-permute-start | bytes 663560 | tf_op jit(solution)/shard_map/ppermute | solution.py:142
  446.7 34.6 %collective-permute-start.7 = (bf16[256,432]{0,1:T(8,128)(2,1)S(1)}, bf16[256,432]{0,1:T(8,128)(2,1)S(1)}, u32[]{:S(2)}, u32[]{:S(2)}) collective-permute-start(bf16[256,432]{0,1:T(8,128)(2,1)S(1)} %get-tuple-element.329), channel_id=1, source_target_pairs={{0,20},{4,24},{8,28},{12,0},{16,4},{20,8},{24,12},{28,16},{1,21},{... | collective-permute-start | bytes 663560 | tf_op jit(solution)/shard_map/ppermute | solution.py:142
  451.6 30.4 %collective-permute-start.8 = (bf16[256,432]{0,1:T(8,128)(2,1)S(1)}, bf16[256,432]{0,1:T(8,128)(2,1)S(1)}, u32[]{:S(2)}, u32[]{:S(2)}) collective-permute-start(bf16[256,432]{0,1:T(8,128)(2,1)S(1)} %get-tuple-element.328), channel_id=1, source_target_pairs={{0,24},{4,28},{8,0},{12,4},{16,8},{20,12},{24,16},{28,20},{1,25},{... | collective-permute-start | bytes 663560 | tf_op jit(solution)/shard_map/ppermute | solution.py:142
  452.9 29.8 %collective-permute-start.9 = (bf16[256,432]{0,1:T(8,128)(2,1)S(1)}, bf16[256,432]{0,1:T(8,128)(2,1)S(1)}, u32[]{:S(2)}, u32[]{:S(2)}) collective-permute-start(bf16[256,432]{0,1:T(8,128)(2,1)S(1)} %get-tuple-element.327), channel_id=1, source_target_pairs={{0,28},{4,0},{8,4},{12,8},{16,12},{20,16},{24,20},{28,24},{1,29},{... | collective-permute-start | bytes 663560 | tf_op jit(solution)/shard_map/ppermute | solution.py:142
  494.1 233.4 %reduce-scatter.14.cloned.1.call-start = ((), (), s32[]{:S(2)}) async-start(), calls=%async_computation.17 | async-start | bytes 5971968 | tf_op jit(solution)/shard_map/reduce_scatter | solution.py:165
  502.3 10.9 %collective-permute-start.20 = (bf16[256,1152]{1,0:T(8,128)(2,1)S(1)}, bf16[256,1152]{1,0:T(8,128)(2,1)S(1)}, u32[]{:S(2)}, u32[]{:S(2)}) collective-permute-start(bf16[256,1152]{1,0:T(8,128)(2,1)S(1)} %bitcast.317), channel_id=1, source_target_pairs={{0,1},{1,2},{2,3},{3,0},{4,5},{5,6},{6,7},{7,4},{8,9},{9,10},{10,1... | collective-permute-start | bytes 1769480 | tf_op jit(solution)/shard_map/ppermute | solution.py:142
  503.7 15.7 %collective-permute-start.21 = (bf16[256,1152]{1,0:T(8,128)(2,1)S(1)}, bf16[256,1152]{1,0:T(8,128)(2,1)S(1)}, u32[]{:S(2)}, u32[]{:S(2)}) collective-permute-start(bf16[256,1152]{1,0:T(8,128)(2,1)S(1)} %bitcast.318), channel_id=1, source_target_pairs={{0,2},{1,3},{2,0},{3,1},{4,6},{5,7},{6,4},{7,5},{8,10},{9,11},{10,... | collective-permute-start | bytes 1769480 | tf_op jit(solution)/shard_map/ppermute | solution.py:142
  503.9 15.5 %collective-permute-start.22 = (bf16[256,1152]{1,0:T(8,128)(2,1)S(1)}, bf16[256,1152]{1,0:T(8,128)(2,1)S(1)}, u32[]{:S(2)}, u32[]{:S(2)}) collective-permute-start(bf16[256,1152]{1,0:T(8,128)(2,1)S(1)} %bitcast.319), channel_id=1, source_target_pairs={{0,3},{1,0},{2,1},{3,2},{4,7},{5,4},{6,5},{7,6},{8,11},{9,8},{10,9... | collective-permute-start | bytes 1769480 | tf_op jit(solution)/shard_map/ppermute | solution.py:142
  533.7 234.2 %reduce-scatter.6.cloned.1.call-start = ((), (), s32[]{:S(2)}) async-start(), calls=%async_computation.10 | async-start | bytes 3317760 | tf_op jit(solution)/shard_map/reduce_scatter | solution.py:165
  552.8 260.5 %reduce-scatter.12.cloned.1.call-start = ((), (), s32[]{:S(2)}) async-start(), calls=%async_computation.16 | async-start | bytes 3686400 | tf_op jit(solution)/shard_map/reduce_scatter | solution.py:158
  556.1 61.7 %collective-permute-start.13 = (bf16[256,576]{0,1:T(8,128)(2,1)S(1)}, bf16[256,576]{0,1:T(8,128)(2,1)S(1)}, u32[]{:S(2)}, u32[]{:S(2)}) collective-permute-start(bf16[256,576]{0,1:T(8,128)(2,1)S(1)} %get-tuple-element.324), channel_id=1, source_target_pairs={{0,4},{4,8},{8,12},{12,16},{16,20},{20,24},{24,28},{28,0},{1,5},{5... | collective-permute-start | bytes 884744 | tf_op jit(solution)/shard_map/ppermute | solution.py:142
  568.8 57.5 %collective-permute-start.14 = (bf16[256,576]{0,1:T(8,128)(2,1)S(1)}, bf16[256,576]{0,1:T(8,128)(2,1)S(1)}, u32[]{:S(2)}, u32[]{:S(2)}) collective-permute-start(bf16[256,576]{0,1:T(8,128)(2,1)S(1)} %get-tuple-element.323), channel_id=1, source_target_pairs={{0,8},{4,12},{8,16},{12,20},{16,24},{20,28},{24,0},{28,4},{1,9},{5... | collective-permute-start | bytes 884744 | tf_op jit(solution)/shard_map/ppermute | solution.py:142
  604.0 31.1 %collective-permute-start.15 = (bf16[256,576]{0,1:T(8,128)(2,1)S(1)}, bf16[256,576]{0,1:T(8,128)(2,1)S(1)}, u32[]{:S(2)}, u32[]{:S(2)}) collective-permute-start(bf16[256,576]{0,1:T(8,128)(2,1)S(1)} %get-tuple-element.322), channel_id=1, source_target_pairs={{0,12},{4,16},{8,20},{12,24},{16,28},{20,0},{24,4},{28,8},{1,13},{... | collective-permute-start | bytes 884744 | tf_op jit(solution)/shard_map/ppermute | solution.py:142
  615.4 27.0 %collective-permute-start.16 = (bf16[256,576]{0,1:T(8,128)(2,1)S(1)}, bf16[256,576]{0,1:T(8,128)(2,1)S(1)}, u32[]{:S(2)}, u32[]{:S(2)}) collective-permute-start(bf16[256,576]{0,1:T(8,128)(2,1)S(1)} %get-tuple-element.321), channel_id=1, source_target_pairs={{0,16},{4,20},{8,24},{12,28},{16,0},{20,4},{24,8},{28,12},{1,17},{... | collective-permute-start | bytes 884744 | tf_op jit(solution)/shard_map/ppermute | solution.py:142
  615.4 27.7 %collective-permute-start.17 = (bf16[256,576]{0,1:T(8,128)(2,1)S(1)}, bf16[256,576]{0,1:T(8,128)(2,1)S(1)}, u32[]{:S(2)}, u32[]{:S(2)}) collective-permute-start(bf16[256,576]{0,1:T(8,128)(2,1)S(1)} %get-tuple-element.320), channel_id=1, source_target_pairs={{0,20},{4,24},{8,28},{12,0},{16,4},{20,8},{24,12},{28,16},{1,21},{... | collective-permute-start | bytes 884744 | tf_op jit(solution)/shard_map/ppermute | solution.py:142
  617.8 26.1 %collective-permute-start.18 = (bf16[256,576]{0,1:T(8,128)(2,1)S(1)}, bf16[256,576]{0,1:T(8,128)(2,1)S(1)}, u32[]{:S(2)}, u32[]{:S(2)}) collective-permute-start(bf16[256,576]{0,1:T(8,128)(2,1)S(1)} %get-tuple-element.319), channel_id=1, source_target_pairs={{0,24},{4,28},{8,0},{12,4},{16,8},{20,12},{24,16},{28,20},{1,25},{... | collective-permute-start | bytes 884744 | tf_op jit(solution)/shard_map/ppermute | solution.py:142
  626.3 22.6 %collective-permute-start.19 = (bf16[256,576]{0,1:T(8,128)(2,1)S(1)}, bf16[256,576]{0,1:T(8,128)(2,1)S(1)}, u32[]{:S(2)}, u32[]{:S(2)}) collective-permute-start(bf16[256,576]{0,1:T(8,128)(2,1)S(1)} %get-tuple-element.318), channel_id=1, source_target_pairs={{0,28},{4,0},{8,4},{12,8},{16,12},{20,16},{24,20},{28,24},{1,29},{... | collective-permute-start | bytes 884744 | tf_op jit(solution)/shard_map/ppermute | solution.py:142
  (53 other events, 575.2 us)
Sparse Core Ops, SparseCore 0:
  203.4 36.2 all-gather.13
  241.3 51.1 all-gather.11
  351.1 38.6 all-gather.17
  413.4 37.5 all-gather.9
  452.6 72.2 all-gather.15
  527.6 55.9 all-gather.19
  586.5 36.7 reduce-scatter.9
  626.9 37.2 reduce-scatter.7
  667.0 60.4 reduce-scatter.13
  730.3 37.6 reduce-scatter.5
  771.6 41.7 reduce-scatter.11
